TPU v7x, 32 devices: a whole 2x2x4 slice. The times are simulated.
32 devices in a mesh: fsdp: 16 (over z, x, core), tp: 2 (over y).
Axes of the slice: x: 2, y: 2, z: 4, core: 2. Of those that a mesh axis runs over, the one named last changes fastest.
Arguments:
- block_input: bfloat16 [3072, 2304], P(('fsdp', 'tp')), may hold values from -6 to 6
- lengths: int32 [16, 9], P('fsdp'), may hold values from 1 to 96, 192 in all within a row
- attention_norm_gain: bfloat16 [2304], P('fsdp'), may hold values from 0.25 to 1.75
- attention_post_gain: bfloat16 [2304], P('fsdp'), may hold values from 0.25 to 1.75
- feedforward_norm_gain: bfloat16 [2304], P('fsdp'), may hold values from 0.25 to 1.75
- feedforward_post_gain: bfloat16 [2304], P('fsdp'), may hold values from 0.25 to 1.75
- query_weight: bfloat16 [2304, 2048], P('fsdp', 'tp'), may hold values from -0.125 to 0.125
- key_weight: bfloat16 [2304, 1024], P('fsdp', 'tp'), may hold values from -0.125 to 0.125
- value_weight: bfloat16 [2304, 1024], P('fsdp', 'tp'), may hold values from -0.125 to 0.125
- output_weight: bfloat16 [2304, 2048], P('fsdp', 'tp'), may hold values from -0.125 to 0.125
- gate_weight: bfloat16 [2304, 9216], P('fsdp', 'tp'), may hold values from -0.125 to 0.125
- up_weight: bfloat16 [2304, 9216], P('fsdp', 'tp'), may hold values from -0.125 to 0.125
- down_weight: bfloat16 [2304, 9216], P('fsdp', 'tp'), may hold values from -0.0625 to 0.0625
- output_cotangent: bfloat16 [3072, 2304], P(('fsdp', 'tp')), may hold values from -6 to 6
Outputs:
- block_output: bfloat16 [3072, 2304], P(('fsdp', 'tp'))
- input_gradient: float32 [3072, 2304], P(('fsdp', 'tp'))
- attention_norm_gain_gradient: float32 [2304], P('fsdp')
- attention_post_gain_gradient: float32 [2304], P('fsdp')
- feedforward_norm_gain_gradient: float32 [2304], P('fsdp')
- feedforward_post_gain_gradient: float32 [2304], P('fsdp')
- query_weight_gradient: float32 [2304, 2048], P('fsdp', 'tp')
- key_weight_gradient: float32 [2304, 1024], P('fsdp', 'tp')
- value_weight_gradient: float32 [2304, 1024], P('fsdp', 'tp')
- output_weight_gradient: float32 [2304, 2048], P('fsdp', 'tp')
- gate_weight_gradient: float32 [2304, 9216], P('fsdp', 'tp')
- up_weight_gradient: float32 [2304, 9216], P('fsdp', 'tp')
- down_weight_gradient: float32 [2304, 9216], P('fsdp', 'tp')
Inputs may be any that keep to these rules, and one draw needn't show every extreme that they name: `lengths`: row g gives the length of group g's prompt (column 0) and of its 8 continuations; each row sums to 192, and its largest entry is 96.
All inputs are finite; a program needn't handle non-finite values.
Results may differ from a plain program's by a relative error of at most 0.017.
Values may be sent and summed in bfloat16 or wider, within the bound.
A program may use at most 512 MiB of HBM per device.

v0:
```python
import math
import jax
import jax.numpy as jnp
from jax import lax
from jax.sharding import PartitionSpec as P

HEAD_SIZE = 256
EPSILON = 1e-06
SOFTCAP = 50.0
NEGATIVE = -1e30


def contract_last(left_rows, right_rows):
    return lax.dot_general(
        left_rows, right_rows, (((1,), (1,)), ((), ())), preferred_element_type=jnp.float32
    )


def contract_first(left_rows, right_rows):
    return lax.dot_general(
        left_rows, right_rows, (((0,), (0,)), ((), ())), preferred_element_type=jnp.float32
    )


def normalize_parts(value_rows):
    inverse = lax.rsqrt(jnp.mean(value_rows * value_rows, axis=-1, keepdims=True) + EPSILON)
    return (value_rows * inverse, inverse)


def norm_backward(unit_rows, inverse, norm_gain, upstream):
    scaled = upstream * norm_gain
    return inverse * (scaled - unit_rows * jnp.mean(scaled * unit_rows, axis=-1, keepdims=True))


def layout(lengths_row, grouped_rows):
    segment_ends = jnp.cumsum(lengths_row)
    segment_starts = segment_ends - lengths_row
    row_index = jnp.arange(grouped_rows, dtype=jnp.int32)
    segment = jnp.sum((row_index[:, None] >= segment_ends[None, :]).astype(jnp.int32), axis=1)
    onehot = segment[:, None] == jnp.arange(lengths_row.shape[0], dtype=jnp.int32)[None, :]
    segment_begin = jnp.sum(jnp.where(onehot, segment_starts[None, :], 0), axis=1)
    prompt_shift = jnp.where(segment > 0, lengths_row[0], 0)
    return (segment, row_index - segment_begin + prompt_shift)


def rotary_tables(position):
    frequency = jnp.exp(
        jnp.arange(HEAD_SIZE // 2, dtype=jnp.float32) * (-2.0 * math.log(10000.0) / HEAD_SIZE)
    )
    angles = position.astype(jnp.float32)[:, None] * frequency[None, :]
    return (jnp.cos(angles), jnp.sin(angles))


def apply_rotary(value_rows, cosine_lookup, sine_lookup):
    half_width = value_rows.shape[-1] // 2
    first_half = value_rows[..., :half_width]
    second_half = value_rows[..., half_width:]
    cosine_part = cosine_lookup[:, None, :]
    sine_part = sine_lookup[:, None, :]
    return jnp.concatenate(
        [
            first_half * cosine_part - second_half * sine_part,
            second_half * cosine_part + first_half * sine_part,
        ],
        axis=-1,
    )


def unrotate(value_rows, cosine_lookup, sine_lookup):
    half_width = value_rows.shape[-1] // 2
    first_half = value_rows[..., :half_width]
    second_half = value_rows[..., half_width:]
    cosine_part = cosine_lookup[:, None, :]
    sine_part = sine_lookup[:, None, :]
    return jnp.concatenate(
        [
            first_half * cosine_part + second_half * sine_part,
            second_half * cosine_part - first_half * sine_part,
        ],
        axis=-1,
    )


def visible(segment):
    row_index = jnp.arange(segment.shape[0], dtype=jnp.int32)
    same_segment = (segment[:, None] == segment[None, :]) & (
        row_index[None, :] <= row_index[:, None]
    )
    from_prompt = (segment[None, :] == 0) & (segment[:, None] > 0)
    return same_segment | from_prompt


def masked_scores(rotated_query, rotated_key, visible_mask):
    raw_scores = jnp.einsum(
        "qgrd,kgd->grqk", rotated_query, rotated_key, preferred_element_type=jnp.float32
    )
    tanh_value = jnp.tanh(raw_scores * HEAD_SIZE ** (-0.5) / SOFTCAP)
    return (jnp.where(visible_mask[None, None], SOFTCAP * tanh_value, NEGATIVE), tanh_value)


def gelu_product(gate_value, up_value):
    return jax.nn.gelu(gate_value, approximate=True) * up_value


def shards(
    block_input,
    lengths,
    attention_norm_gain,
    attention_post_gain,
    feedforward_norm_gain,
    feedforward_post_gain,
    query_weight,
    key_weight,
    value_weight,
    output_weight,
    gate_weight,
    up_weight,
    down_weight,
    output_cotangent,
):
    query_full, key_full, value_full, output_full, gain_one, gain_two = (
        lax.all_gather(query_weight, "fsdp", axis=0, tiled=True),
        lax.all_gather(key_weight, "fsdp", axis=0, tiled=True),
        lax.all_gather(value_weight, "fsdp", axis=0, tiled=True),
        lax.all_gather(output_weight, "fsdp", axis=0, tiled=True),
        lax.all_gather(attention_norm_gain, "fsdp", axis=0, tiled=True),
        lax.all_gather(attention_post_gain, "fsdp", axis=0, tiled=True),
    )
    gate_full, up_full, down_full, gain_three, gain_four = (
        lax.all_gather(gate_weight, "fsdp", axis=0, tiled=True),
        lax.all_gather(up_weight, "fsdp", axis=0, tiled=True),
        lax.all_gather(down_weight, "fsdp", axis=0, tiled=True),
        lax.all_gather(feedforward_norm_gain, "fsdp", axis=0, tiled=True),
        lax.all_gather(feedforward_post_gain, "fsdp", axis=0, tiled=True),
    )
    gain_one = gain_one.astype(jnp.float32)
    gain_two = gain_two.astype(jnp.float32)
    gain_three = gain_three.astype(jnp.float32)
    gain_four = gain_four.astype(jnp.float32)
    rows_local = block_input.shape[0]
    grouped_rows = rows_local * lax.axis_size("tp")
    segment, position = layout(lengths[0], grouped_rows)
    cosine_lookup, sine_lookup = rotary_tables(position)
    visible_mask = visible(segment)
    residual = block_input.astype(jnp.float32)
    unit_one, inverse_one = normalize_parts(residual)
    normed_local = (unit_one * gain_one).astype(jnp.bfloat16)
    normed = lax.all_gather(normed_local, "tp", axis=0, tiled=True)
    query_raw = jnp.dot(normed, query_full, preferred_element_type=jnp.float32)
    key_raw = jnp.dot(normed, key_full, preferred_element_type=jnp.float32)
    value_raw = jnp.dot(normed, value_full, preferred_element_type=jnp.float32)
    heads_local = query_raw.shape[1] // HEAD_SIZE
    kv_local = key_raw.shape[1] // HEAD_SIZE
    repeat_heads = heads_local // kv_local
    rotated_query = apply_rotary(
        query_raw.reshape(grouped_rows, heads_local, HEAD_SIZE), cosine_lookup, sine_lookup
    ).astype(jnp.bfloat16)
    rotated_query = rotated_query.reshape(grouped_rows, kv_local, repeat_heads, HEAD_SIZE)
    rotated_key = apply_rotary(
        key_raw.reshape(grouped_rows, kv_local, HEAD_SIZE), cosine_lookup, sine_lookup
    ).astype(jnp.bfloat16)
    value_reduced = value_raw.astype(jnp.bfloat16).reshape(grouped_rows, kv_local, HEAD_SIZE)
    capped, tanh_value = masked_scores(rotated_query, rotated_key, visible_mask)
    row_peak = jnp.max(capped, axis=-1, keepdims=True)
    log_total = row_peak + jnp.log(jnp.sum(jnp.exp(capped - row_peak), axis=-1, keepdims=True))
    softmax_probs = jnp.exp(capped - log_total)
    mixed_heads = jnp.einsum(
        "grqk,kgd->qgrd",
        softmax_probs.astype(jnp.bfloat16),
        value_reduced,
        preferred_element_type=jnp.float32,
    )
    attended = mixed_heads.reshape(grouped_rows, heads_local * HEAD_SIZE).astype(jnp.bfloat16)
    row_piece = attended
    branch_one = lax.psum_scatter(
        contract_last(row_piece, output_full), "tp", scatter_dimension=0, tiled=True
    )
    unit_two, inverse_two = normalize_parts(branch_one)
    middle = residual + unit_two * gain_two
    unit_three, inverse_three = normalize_parts(middle)
    feed_local = (unit_three * gain_three).astype(jnp.bfloat16)
    feed_input = lax.all_gather(feed_local, "tp", axis=0, tiled=True)
    gate_value = jnp.dot(feed_input, gate_full, preferred_element_type=jnp.float32)
    up_value = jnp.dot(feed_input, up_full, preferred_element_type=jnp.float32)
    hidden = gelu_product(gate_value, up_value).astype(jnp.bfloat16)
    row_piece = hidden
    branch_two = lax.psum_scatter(
        contract_last(row_piece, down_full), "tp", scatter_dimension=0, tiled=True
    )
    unit_four, inverse_four = normalize_parts(branch_two)
    block_output = (middle + unit_four * gain_four).astype(jnp.bfloat16)
    upstream = output_cotangent.astype(jnp.float32)
    gain_four_grad = jnp.sum(upstream * unit_four, axis=0)
    branch_two_grad = norm_backward(unit_four, inverse_four, gain_four, upstream).astype(
        jnp.bfloat16
    )
    held_back = lax.optimization_barrier(
        (
            query_weight,
            key_weight,
            value_weight,
            output_weight,
            gate_weight,
            up_weight,
            down_weight,
            branch_two_grad,
        )
    )
    query_full, key_full, value_full, output_full, gate_full, up_full, down_full = (
        lax.all_gather(held_back[0], "fsdp", axis=0, tiled=True),
        lax.all_gather(held_back[1], "fsdp", axis=0, tiled=True),
        lax.all_gather(held_back[2], "fsdp", axis=0, tiled=True),
        lax.all_gather(held_back[3], "fsdp", axis=0, tiled=True),
        lax.all_gather(held_back[4], "fsdp", axis=0, tiled=True),
        lax.all_gather(held_back[5], "fsdp", axis=0, tiled=True),
        lax.all_gather(held_back[6], "fsdp", axis=0, tiled=True),
    )
    branch_two_grad = held_back[7]
    feed_grad_rows = lax.all_gather(branch_two_grad, "tp", axis=0, tiled=True)
    hidden_grad = jnp.dot(feed_grad_rows, down_full, preferred_element_type=jnp.float32)
    unused_out, pullback = jax.vjp(gelu_product, gate_value, up_value)
    gate_grad, up_grad = pullback(hidden_grad)
    gate_up_grad = jnp.concatenate(
        [gate_grad.astype(jnp.bfloat16), up_grad.astype(jnp.bfloat16)], axis=1
    )
    feed_split = gate_full.shape[1]
    shard_rows = query_weight.shape[0]
    left_rows = feed_input
    feed_weight_grads = lax.psum_scatter(
        jnp.concatenate(
            [contract_first(left_rows, gate_up_grad), contract_first(feed_grad_rows, hidden)],
            axis=1,
        ),
        "fsdp",
        scatter_dimension=0,
        tiled=True,
    )
    row_piece = gate_up_grad
    normed_three_grad = lax.psum_scatter(
        contract_last(row_piece[:, :feed_split], gate_full)
        + contract_last(row_piece[:, feed_split:], up_full),
        "tp",
        scatter_dimension=0,
        tiled=True,
    )
    gain_three_grad = jnp.sum(normed_three_grad * unit_three, axis=0)
    middle_grad = upstream + norm_backward(unit_three, inverse_three, gain_three, normed_three_grad)
    gain_two_grad = jnp.sum(middle_grad * unit_two, axis=0)
    branch_one_grad = norm_backward(unit_two, inverse_two, gain_two, middle_grad).astype(
        jnp.bfloat16
    )
    attention_grad_rows = lax.all_gather(branch_one_grad, "tp", axis=0, tiled=True)
    mixed_grad = jnp.dot(
        attention_grad_rows, output_full, preferred_element_type=jnp.float32
    ).astype(jnp.bfloat16)
    mixed_grad = mixed_grad.reshape(grouped_rows, kv_local, repeat_heads, HEAD_SIZE)
    capped_again, tanh_again = masked_scores(rotated_query, rotated_key, visible_mask)
    probs_again = jnp.exp(capped_again - log_total)
    value_grad = jnp.einsum(
        "grqk,qgrd->kgd",
        probs_again.astype(jnp.bfloat16),
        mixed_grad,
        preferred_element_type=jnp.float32,
    )
    probs_grad = jnp.einsum(
        "qgrd,kgd->grqk", mixed_grad, value_reduced, preferred_element_type=jnp.float32
    )
    score_grad = probs_again * (
        probs_grad - jnp.sum(probs_again * probs_grad, axis=-1, keepdims=True)
    )
    raw_grad = (score_grad * (1.0 - tanh_again * tanh_again) * HEAD_SIZE ** (-0.5)).astype(
        jnp.bfloat16
    )
    query_grad = jnp.einsum(
        "grqk,kgd->qgrd", raw_grad, rotated_key, preferred_element_type=jnp.float32
    )
    key_grad = jnp.einsum(
        "grqk,qgrd->kgd", raw_grad, rotated_query, preferred_element_type=jnp.float32
    )
    query_grad = unrotate(
        query_grad.reshape(grouped_rows, heads_local, HEAD_SIZE), cosine_lookup, sine_lookup
    )
    key_grad = unrotate(key_grad, cosine_lookup, sine_lookup)
    projected_grad = jnp.concatenate(
        [
            query_grad.reshape(grouped_rows, heads_local * HEAD_SIZE).astype(jnp.bfloat16),
            key_grad.reshape(grouped_rows, kv_local * HEAD_SIZE).astype(jnp.bfloat16),
            value_grad.reshape(grouped_rows, kv_local * HEAD_SIZE).astype(jnp.bfloat16),
        ],
        axis=1,
    )
    query_width = query_full.shape[1]
    key_width = key_full.shape[1]
    left_rows = normed
    attention_weight_grads = lax.psum_scatter(
        jnp.concatenate(
            [
                contract_first(left_rows, projected_grad),
                contract_first(attention_grad_rows, attended),
            ],
            axis=1,
        ),
        "fsdp",
        scatter_dimension=0,
        tiled=True,
    )
    row_piece = projected_grad
    total = contract_last(row_piece[:, :query_width], query_full)
    total = total + contract_last(row_piece[:, query_width : query_width + key_width], key_full)
    normed_one_grad = lax.psum_scatter(
        (total + contract_last(row_piece[:, query_width + key_width :], value_full)).astype(
            jnp.bfloat16
        ),
        "tp",
        scatter_dimension=0,
        tiled=True,
    ).astype(jnp.float32)
    gain_one_grad = jnp.sum(normed_one_grad * unit_one, axis=0)
    input_gradient = middle_grad + norm_backward(unit_one, inverse_one, gain_one, normed_one_grad)
    gain_sums = lax.psum(
        (gain_one_grad, gain_two_grad, gain_three_grad, gain_four_grad), ("fsdp", "tp")
    )
    offset = lax.axis_index("fsdp") * shard_rows
    gain_shards = [
        lax.dynamic_slice_in_dim(total_sum, offset, shard_rows) for total_sum in gain_sums
    ]
    value_start = query_width + key_width
    output_start = value_start + key_width
    return (
        block_output,
        input_gradient,
        gain_shards[0],
        gain_shards[1],
        gain_shards[2],
        gain_shards[3],
        attention_weight_grads[:, :query_width],
        attention_weight_grads[:, query_width:value_start],
        attention_weight_grads[:, value_start:output_start],
        attention_weight_grads[:, output_start:],
        feed_weight_grads[:, :feed_split],
        feed_weight_grads[:, feed_split : 2 * feed_split],
        feed_weight_grads[:, 2 * feed_split :],
    )


def solution(mesh):
    placed = (
        P(("fsdp", "tp"), None),
        P("fsdp", None),
        P("fsdp"),
        P("fsdp"),
        P("fsdp"),
        P("fsdp"),
        P("fsdp", "tp"),
        P("fsdp", "tp"),
        P("fsdp", "tp"),
        P("fsdp", "tp"),
        P("fsdp", "tp"),
        P("fsdp", "tp"),
        P("fsdp", "tp"),
        P(("fsdp", "tp"), None),
    )
    return jax.shard_map(
        shards,
        mesh=mesh,
        in_specs=placed,
        out_specs=(
            P(("fsdp", "tp"), None),
            P(("fsdp", "tp"), None),
            P("fsdp"),
            P("fsdp"),
            P("fsdp"),
            P("fsdp"),
            P("fsdp", "tp"),
            P("fsdp", "tp"),
            P("fsdp", "tp"),
            P("fsdp", "tp"),
            P("fsdp", "tp"),
            P("fsdp", "tp"),
            P("fsdp", "tp"),
        ),
        check_vma=False,
    )
```

profile of v0, /device:TPU:0, one launch (start us, length us, event | category | flops | bytes accessed | tf_op | source)
XLA Modules:
  0.0 2708.5 jit_solution(12363852051479386329)
XLA Ops:
  10.0 1.2 dynamic-slice
  15.4 63.9 %all-reduce.5 = (bf16[2304]{0:T(1024)(128)(2,1)S(1)}, bf16[2304]{0:T(1024)(128)(2,1)S(1)}, bf16[2304]{0:T(1024)(128)(2,1)S(1)}, bf16[2304]{0:T(1024)(128)(2,1)S(1)}) all-reduce(bf16[2304]{0:T(1024)(128)(2,1)S(1)} %dynamic-update-slice, bf16[2304]{0:T(1024)(128)(2,1)S(1)} %dynamic-update-slice.1, ...), channel_id=1, replica_groups=mesh['fsdp'=16,'tp'=2] {'fsdp'}, use_global_device_ids=true, to_apply=%add | all-reduce | flops 9216 | bytes 36864
  80.9 1.2 fusion.37
  82.1 1.2 fusion.34
  83.3 9.0 all_gather.67
  93.0 2.3 fusion.107
  95.6 3.4 all-gather.15.cloned.1.call-done
  99.0 2.3 convolution_convert_fusion.2
  101.6 51.6 %all-gather.19.cloned.1.call-done = bf16[2304,1024]{1,0:T(8,128)(2,1)} async-done(((bf16[144,1024]{1,0:T(8,128)(2,1)}), bf16[2304,1024]{1,0:T(8,128)(2,1)}) %all-gather.19.cloned.1.call-update) | async-done | bytes 4718608 | tf_op jit(solution)/shard_map/all_gather | solution.py:122
  153.2 3.4 fusion.108
  159.3 47.7 %all-gather.21.cloned.1.call-done = bf16[2304,1024]{1,0:T(8,128)(2,1)} async-done(((bf16[144,1024]{1,0:T(8,128)(2,1)}), bf16[2304,1024]{1,0:T(8,128)(2,1)}) %all-gather.21.cloned.1.call-update) | async-done | bytes 4718608 | tf_op jit(solution)/shard_map/all_gather | solution.py:125
  207.0 5.2 fusion.109
  214.4 24.9 reduce-scatter.9.cloned.1.call-done
  239.3 1.3 multiply_reduce_fusion.6
  240.6 1.5 multiply_reduce_fusion.5
  242.3 12.7 all_gather.74
  255.1 95.7 %all-gather.23.cloned.1.call-done = bf16[2304,4608]{1,0:T(8,128)(2,1)} async-done(((bf16[144,4608]{1,0:T(8,128)(2,1)}), bf16[2304,4608]{1,0:T(8,128)(2,1)}) %all-gather.23.cloned.1.call-update) | async-done | bytes 21233680 | tf_op jit(solution)/shard_map/all_gather | solution.py:130
  350.8 11.4 fusion.110
  362.2 100.3 %all-gather.25.cloned.1.call-done = bf16[2304,4608]{1,0:T(8,128)(2,1)} async-done(((bf16[144,4608]{1,0:T(8,128)(2,1)}), bf16[2304,4608]{1,0:T(8,128)(2,1)}) %all-gather.25.cloned.1.call-update) | async-done | bytes 21233680 | tf_op jit(solution)/shard_map/all_gather | solution.py:131
  462.4 14.7 multiply_convert_fusion.1
  477.2 96.9 %all-gather.27.cloned.1.call-done = bf16[2304,4608]{1,0:T(8,128)(2,1)} async-done(((bf16[144,4608]{1,0:T(8,128)(2,1)}), bf16[2304,4608]{1,0:T(8,128)(2,1)}) %all-gather.27.cloned.1.call-update) | async-done | bytes 21233680 | tf_op jit(solution)/shard_map/all_gather | solution.py:132
  574.0 12.6 fusion.111
  586.8 28.4 %reduce-scatter.11.cloned.1.call-done = f32[96,2304]{1,0:T(8,128)} async-done(((f32[192,2304]{1,0:T(8,128)}), f32[96,2304]{1,0:T(8,128)}) %reduce-scatter.11.cloned.1.call-update) | async-done | bytes 884752 | tf_op jit(solution)/shard_map/reduce_scatter | solution.py:187
  615.1 1.3 multiply_reduce_fusion.4
  616.5 2.0 fusion.38
  618.5 2.2 fusion.31
  622.2 12.9 all_gather.79
  635.1 95.9 %all-gather.29.cloned.1.call-done = bf16[2304,4608]{1,0:T(8,128)(2,1)} async-done(((bf16[144,4608]{1,0:T(8,128)(2,1)}), bf16[2304,4608]{1,0:T(8,128)(2,1)}) %all-gather.29.cloned.1.call-update) | async-done | bytes 21233680 | tf_op jit(solution)/shard_map/all_gather | solution.py:216
  731.0 14.2 multiply_convert_fusion
  745.2 97.4 %all-gather.31.cloned.1.call-done = bf16[2304,4608]{1,0:T(8,128)(2,1)} async-done(((bf16[144,4608]{1,0:T(8,128)(2,1)}), bf16[2304,4608]{1,0:T(8,128)(2,1)}) %all-gather.31.cloned.1.call-update) | async-done | bytes 21233680 | tf_op jit(solution)/shard_map/all_gather | solution.py:214
  842.6 12.6 fusion.112
  855.2 98.8 %all-gather.33.cloned.1.call-done = bf16[2304,4608]{1,0:T(8,128)(2,1)} async-done(((bf16[144,4608]{1,0:T(8,128)(2,1)}), bf16[2304,4608]{1,0:T(8,128)(2,1)}) %all-gather.33.cloned.1.call-update) | async-done | bytes 21233680 | tf_op jit(solution)/shard_map/all_gather | solution.py:215
  954.1 13.1 convolution_add_fusion.2
  969.6 26.1 reduce-scatter.13.cloned.1.call-done
  995.7 2.0 multiply_reduce_fusion
  997.7 2.2 multiply_reduce_fusion.1
  1000.8 12.6 all_gather.83
  1013.4 37.5 %all-gather.35.cloned.1.call-done = bf16[2304,1024]{1,0:T(8,128)(2,1)} async-done(((bf16[144,1024]{1,0:T(8,128)(2,1)}), bf16[2304,1024]{1,0:T(8,128)(2,1)}) %all-gather.35.cloned.1.call-update) | async-done | bytes 4718608 | tf_op jit(solution)/shard_map/all_gather | solution.py:213
  1051.0 4.2 convolution_convert_fusion
  1055.1 1.3 reshape.272
  1057.6 1.2 convolution_bitcast_fusion
  1058.8 2.3 convolution_bitcast_fusion.2
  1061.9 3.1 fusion.39
  1067.1 37.7 %all-gather.37.cloned.1.call-done = bf16[2304,1024]{1,0:T(8,128)(2,1)} async-done(((bf16[144,1024]{1,0:T(8,128)(2,1)}), bf16[2304,1024]{1,0:T(8,128)(2,1)}) %all-gather.37.cloned.1.call-update) | async-done | bytes 4718608 | tf_op jit(solution)/shard_map/all_gather | solution.py:210
  1104.8 5.3 fusion.113
  1110.1 37.7 %all-gather.39.cloned.1.call-done = bf16[2304,512]{1,0:T(8,128)(2,1)} async-done(((bf16[144,512]{1,0:T(8,128)(2,1)}), bf16[2304,512]{1,0:T(8,128)(2,1)}) %all-gather.39.cloned.1.call-update) | async-done | bytes 2359312 | tf_op jit(solution)/shard_map/all_gather | solution.py:211
  1147.8 3.2 convolution_add_fusion.1
  1151.1 5.0 fusion.114
  1156.1 8.0 fusion.44
  1164.1 26.9 all-gather.41.cloned.1.call-done
  1191.0 3.5 fusion.1
  1194.6 18.8 pad_maximum_fusion.1
  1213.4 27.7 %copy.111 = f32[2304,3072]{1,0:T(8,128)} copy(f32[2304,3072]{0,1:T(8,128)} %pad_maximum_fusion.1) | data formatting | bytes 56623104
  1242.3 27.8 %fusion.115 = f32[2304,4608]{1,0:T(8,128)} fusion(bf16[192,2304]{1,0:T(8,128)(2,1)S(1)} %copy-done.6, bf16[192,4608]{1,0:T(8,128)(2,1)} %get-tuple-element.129), kind=kOutput, calls=%fused_computation.171 | convolution fusion | flops 4076863488 | bytes 45121536 | tf_op jit(solution)/shard_map/dot_general | solution.py:20
  1270.1 32.5 %fusion.9 = f32[2304,9216]{1,0:T(8,128)} fusion(bf16[192,2304]{1,0:T(8,128)(2,1)S(1)} %copy-done.9, bf16[192,4608]{1,0:T(8,128)(2,1)S(1)} %copy-done.17, bf16[192,4608]{1,0:T(8,128)(2,1)S(1)} %copy-done.18), kind=kOutput, calls=%fused_computation.16 | convolution fusion | flops 8160804864 | bytes 89358336 | tf_op jit(solution)/shard_map/dot_general | solution.py:20
  1302.7 85.6 %pad_maximum_fusion = f32[2304,13824]{1,0:T(8,128)} fusion(f32[2304,4608]{1,0:T(8,128)} %fusion.115, f32[2304,9216]{1,0:T(8,128)} %fusion.9), kind=kLoop, calls=%fused_computation.1 | loop fusion | flops 31850496 | bytes 254803968 | tf_op jit(solution)/shard_map/concatenate | solution.py:230
  1389.3 1.4 fusion.36
  1390.7 40.4 %all-reduce.4 = (f32[2304]{0:T(1024)S(1)}, f32[2304]{0:T(1024)S(1)}, f32[2304]{0:T(1024)S(1)}, f32[2304]{0:T(1024)S(1)}) all-reduce(f32[2304]{0:T(1024)S(1)} %get-tuple-element.87, f32[2304]{0:T(1024)S(1)} %copy-done.40, f32[2304]{0:T(1024)S(1)} %copy-done.39, f32[2304]{0:T(1024)S(1)} %copy-done.38), channel_id=1, replica_groups=mesh['fsdp'=16,'tp'=2] {'fsdp','tp'}, use_global_device_ids=true, to_apply=%region_19.20 | all-reduce | flops 9216 | bytes 73728 | tf_op jit(solution)/shard_map/psum | solution.py:320
  1433.7 2.2 fusion.33
  1436.0 76.9 %reduce-scatter.19.cloned.1.call-done = f32[144,3072]{1,0:T(8,128)} async-done(((f32[2304,3072]{1,0:T(8,128)}), f32[144,3072]{1,0:T(8,128)}) %reduce-scatter.19.cloned.1.call-update) | async-done | bytes 1769488
  1512.9 1.9 fusion.104
  1514.8 2.4 fusion.103
  1517.2 1177.5 %reduce-scatter.17.cloned.1.call-done = f32[144,13824]{1,0:T(8,128)} async-done(((f32[2304,13824]{1,0:T(8,128)}), f32[144,13824]{1,0:T(8,128)}) %reduce-scatter.17.cloned.1.call-update) | async-done | bytes 7962640 | tf_op jit(solution)/shard_map/reduce_scatter | solution.py:229
  2694.7 6.8 fusion.102
  (196 shorter events, 27.1 us)
Async XLA Ops:
  7.2 85.1 %copy-start.47 = (s32[1,9]{1,0:T(1,128)S(1)}, s32[1,9]{1,0:T(1,128)}, u32[]{:S(2)}) copy-start(s32[1,9]{1,0:T(1,128)} %param.15) | copy-start | bytes 112
  7.2 85.8 %all-gather.17.cloned.1.call-start = ((), (), s32[]{:S(2)}) async-start(), calls=%async_computation.7 | async-start | bytes 2506752 | tf_op jit(solution)/shard_map/all_gather | solution.py:123
  7.9 91.1 %all-gather.15.cloned.1.call-start = ((), (), s32[]{:S(2)}) async-start(), calls=%async_computation.6 | async-start | bytes 2506752 | tf_op jit(solution)/shard_map/all_gather | solution.py:124
  8.7 144.5 %all-gather.19.cloned.1.call-start = ((), (), s32[]{:S(2)}) async-start(), calls=%async_computation.8 | async-start | bytes 5013504 | tf_op jit(solution)/shard_map/all_gather | solution.py:122
  9.4 197.6 %all-gather.21.cloned.1.call-start = ((), (), s32[]{:S(2)}) async-start(), calls=%async_computation.9 | async-start | bytes 5013504 | tf_op jit(solution)/shard_map/all_gather | solution.py:125
  10.0 229.3 %reduce-scatter.9.cloned.1.call-start = ((), (), s32[]{:S(2)}) async-start(), calls=%async_computation.10 | async-start | bytes 2654208 | tf_op jit(solution)/shard_map/reduce_scatter | solution.py:175
  79.2 13.7 copy-start.27
  82.1 13.4 copy-start.41
  92.5 65.4 %copy-start.29 = (pred[192,192]{0,1:T(8,128)(4,1)}, pred[192,192]{0,1:T(8,128)(4,1)S(1)}, u32[]{:S(2)}) copy-start(pred[192,192]{0,1:T(8,128)(4,1)S(1)} %fusion.77) | copy-start | bytes 110596
  92.9 64.0 %copy-start.10 = (f32[192,128]{1,0:T(8,128)}, f32[192,128]{1,0:T(8,128)S(1)}, u32[]{:S(2)}) copy-start(f32[192,128]{1,0:T(8,128)S(1)} %get-tuple-element.125) | copy-start | bytes 294916
  92.9 64.0 %copy-start.12 = (f32[192,128]{1,0:T(8,128)}, f32[192,128]{1,0:T(8,128)S(1)}, u32[]{:S(2)}) copy-start(f32[192,128]{1,0:T(8,128)S(1)} %get-tuple-element.126) | copy-start | bytes 294916
  101.3 56.6 %copy-start.25 = (bf16[192,2,256]{2,1,0:T(2,128)(2,1)}, bf16[192,2,256]{2,1,0:T(2,128)(2,1)S(1)}, u32[]{:S(2)}) copy-start(bf16[192,2,256]{2,1,0:T(2,128)(2,1)S(1)} %reshape.267) | copy-start | bytes 589828
  101.6 55.7 %copy-start.35 = (bf16[192,2,128]{2,0,1:T(8,128)(2,1)}, bf16[192,2,128]{2,0,1:T(8,128)(2,1)S(1)}, u32[]{:S(2)}) copy-start(bf16[192,2,128]{2,0,1:T(8,128)(2,1)S(1)} %get-tuple-element.121) | copy-start | bytes 294916
  101.6 55.7 %copy-start.37 = (bf16[192,2,128]{2,0,1:T(8,128)(2,1)}, bf16[192,2,128]{2,0,1:T(8,128)(2,1)S(1)}, u32[]{:S(2)}) copy-start(bf16[192,2,128]{2,0,1:T(8,128)(2,1)S(1)} %get-tuple-element.122) | copy-start | bytes 294916
  157.2 1.1 copy-start.31
  157.3 1.1 copy-start.32
  157.9 54.3 %copy-start.45 = (f32[2,2,192]{2,1,0:T(2,128)}, f32[2,2,192]{2,1,0:T(2,128)S(1)}, u32[]{:S(2)}) copy-start(f32[2,2,192]{2,1,0:T(2,128)S(1)} %log_add_fusion) | copy-start | bytes 9220
  159.2 53.0 %copy-start.19 = (bf16[192,1024]{1,0:T(8,128)(2,1)}, bf16[192,1024]{1,0:T(8,128)(2,1)S(1)}, u32[]{:S(2)}) copy-start(bf16[192,1024]{1,0:T(8,128)(2,1)S(1)} %convert_element_type.109) | copy-start | bytes 1179652
  212.2 28.4 %copy-start.1 = (bf16[96,2304]{1,0:T(8,128)(2,1)S(1)}, bf16[96,2304]{1,0:T(8,128)(2,1)}, u32[]{:S(2)}) copy-start(bf16[96,2304]{1,0:T(8,128)(2,1)} %param.14) | copy-start | bytes 1327108
  212.3 138.5 %all-gather.23.cloned.1.call-start = ((), (), s32[]{:S(2)}) async-start(), calls=%async_computation.11 | async-start | bytes 22560768 | tf_op jit(solution)/shard_map/all_gather | solution.py:130
  212.8 249.6 %all-gather.25.cloned.1.call-start = ((), (), s32[]{:S(2)}) async-start(), calls=%async_computation.12 | async-start | bytes 22560768 | tf_op jit(solution)/shard_map/all_gather | solution.py:131
  213.6 360.4 %all-gather.27.cloned.1.call-start = ((), (), s32[]{:S(2)}) async-start(), calls=%async_computation.13 | async-start | bytes 22560768 | tf_op jit(solution)/shard_map/all_gather | solution.py:132
  214.3 400.8 %reduce-scatter.11.cloned.1.call-start = ((), (), s32[]{:S(2)}) async-start(), calls=%async_computation.14 | async-start | bytes 2654208 | tf_op jit(solution)/shard_map/reduce_scatter | solution.py:187
  214.4 27.8 %copy-start.33 = (f32[2304]{0:T(1024)}, f32[2304]{0:T(1024)S(1)}, u32[]{:S(2)}) copy-start(f32[2304]{0:T(1024)S(1)} %convert_element_type.111) | copy-start | bytes 27652
  240.6 1.6 copy-start.43
  255.1 207.4 %copy-start.8 = (bf16[192,2304]{1,0:T(8,128)(2,1)}, bf16[192,2304]{1,0:T(8,128)(2,1)S(1)}, u32[]{:S(2)}) copy-start(bf16[192,2304]{1,0:T(8,128)(2,1)S(1)} %all_gather.74) | copy-start | bytes 2654212
  574.0 42.5 %copy-start.7 = (bf16[96,2304]{1,0:T(8,128)(2,1)S(1)}, bf16[96,2304]{1,0:T(8,128)(2,1)}, u32[]{:S(2)}) copy-start(bf16[96,2304]{1,0:T(8,128)(2,1)} %param.27) | copy-start | bytes 1327108
  586.7 144.3 %all-gather.29.cloned.1.call-start = ((), (), s32[]{:S(2)}) async-start(), calls=%async_computation.15 | async-start | bytes 22560768 | tf_op jit(solution)/shard_map/all_gather | solution.py:216
  620.8 221.8 %all-gather.31.cloned.1.call-start = ((), (), s32[]{:S(2)}) async-start(), calls=%async_computation.16 | async-start | bytes 22560768 | tf_op jit(solution)/shard_map/all_gather | solution.py:214
  621.5 332.5 %all-gather.33.cloned.1.call-start = ((), (), s32[]{:S(2)}) async-start(), calls=%async_computation.17 | async-start | bytes 22560768 | tf_op jit(solution)/shard_map/all_gather | solution.py:215
  622.1 373.6 %reduce-scatter.13.cloned.1.call-start = ((), (), s32[]{:S(2)}) async-start(), calls=%async_computation.18 | async-start | bytes 2654208 | tf_op jit(solution)/shard_map/reduce_scatter | solution.py:239
  635.1 110.1 %copy-start.5 = (bf16[192,2304]{1,0:T(8,128)(2,1)}, bf16[192,2304]{1,0:T(8,128)(2,1)S(1)}, u32[]{:S(2)}) copy-start(bf16[192,2304]{1,0:T(8,128)(2,1)S(1)} %all_gather.79) | copy-start | bytes 2654212
  954.1 41.6 %copy-start.34 = (f32[2304]{0:T(1024)S(1)}, f32[2304]{0:T(1024)}, u32[]{:S(2)}) copy-start(f32[2304]{0:T(1024)} %copy-done.33) | copy-start | bytes 27652
  967.2 30.5 %copy-start = (f32[96,2304]{1,0:T(8,128)S(1)}, f32[96,2304]{1,0:T(8,128)}, u32[]{:S(2)}) copy-start(f32[96,2304]{1,0:T(8,128)} %reduce-scatter.9.cloned.1.call-done) | copy-start | bytes 2654212
  967.2 30.5 %copy-start.44 = (f32[96]{0:T(128)S(1)}, f32[96]{0:T(128)}, u32[]{:S(2)}) copy-start(f32[96]{0:T(128)} %copy-done.43) | copy-start | bytes 1156
  967.2 83.7 %all-gather.35.cloned.1.call-start = ((), (), s32[]{:S(2)}) async-start(), calls=%async_computation.19 | async-start | bytes 5013504 | tf_op jit(solution)/shard_map/all_gather | solution.py:213
  967.8 137.0 %all-gather.37.cloned.1.call-start = ((), (), s32[]{:S(2)}) async-start(), calls=%async_computation.20 | async-start | bytes 5013504 | tf_op jit(solution)/shard_map/all_gather | solution.py:210
  968.4 179.4 %all-gather.39.cloned.1.call-start = ((), (), s32[]{:S(2)}) async-start(), calls=%async_computation.21 | async-start | bytes 2506752 | tf_op jit(solution)/shard_map/all_gather | solution.py:211
  969.0 222.0 %all-gather.41.cloned.1.call-start = ((), (), s32[]{:S(2)}) async-start(), calls=%async_computation.22 | async-start | bytes 2506752 | tf_op jit(solution)/shard_map/all_gather | solution.py:212
  969.6 418.8 %reduce-scatter.15.cloned.1.call-start = ((), (), s32[]{:S(2)}) async-start(), calls=%async_computation.23 | async-start | bytes 1327104 | tf_op jit(solution)/shard_map/reduce_scatter | solution.py:310
  1013.4 43.0 %copy-start.24 = (f32[2,192,192,2]{2,1,3,0:T(8,128)S(1)}, f32[2,192,192,2]{2,1,3,0:T(8,128)}, u32[]{:S(2)}) copy-start(f32[2,192,192,2]{2,1,3,0:T(8,128)} %copy-done.23) | copy-start | bytes 1769476
  1013.4 43.0 %copy-start.30 = (pred[192,192]{0,1:T(8,128)(4,1)S(1)}, pred[192,192]{0,1:T(8,128)(4,1)}, u32[]{:S(2)}) copy-start(pred[192,192]{0,1:T(8,128)(4,1)} %copy-done.29) | copy-start | bytes 110596
  1013.4 43.0 %copy-start.46 = (f32[2,2,192]{2,1,0:T(2,128)S(1)}, f32[2,2,192]{2,1,0:T(2,128)}, u32[]{:S(2)}) copy-start(f32[2,2,192]{2,1,0:T(2,128)} %copy-done.45) | copy-start | bytes 9220
  1013.4 44.2 %copy-start.26 = (bf16[192,2,256]{2,1,0:T(2,128)(2,1)S(1)}, bf16[192,2,256]{2,1,0:T(2,128)(2,1)}, u32[]{:S(2)}) copy-start(bf16[192,2,256]{2,1,0:T(2,128)(2,1)} %copy-done.25) | copy-start | bytes 589828
  1056.4 4.7 copy-start.11
  1056.5 4.7 copy-start.13
  1056.9 5.1 copy-start.36
  1067.1 43.0 %copy-start.21 = (bf16[24,8,4,256]{3,1,2,0:T(8,128)(2,1)}, bf16[24,8,4,256]{3,1,2,0:T(8,128)(2,1)S(1)}, u32[]{:S(2)}) copy-start(bf16[24,8,4,256]{3,1,2,0:T(8,128)(2,1)S(1)} %copy.123) | copy-start | bytes 1179652
  1147.8 3.2 copy-start.20
  1151.1 5.0 copy-start.14
  1151.1 5.0 copy-start.16
  1151.1 5.0 copy-start.22
  1156.1 34.9 %copy-start.15 = (bf16[2,24,8,256]{3,2,0,1:T(8,128)(2,1)S(1)}, bf16[2,24,8,256]{3,2,0,1:T(8,128)(2,1)}, u32[]{:S(2)}) copy-start(bf16[2,24,8,256]{3,2,0,1:T(8,128)(2,1)} %copy.122) | copy-start | bytes 589828
  1194.6 318.4 %reduce-scatter.19.cloned.1.call-start = ((), (), s32[]{:S(2)}) async-start(), calls=%async_computation.25 | async-start | bytes 30081024
  1241.2 1.2 copy-start.6
  1241.2 28.9 %copy-start.9 = (bf16[192,2304]{1,0:T(8,128)(2,1)S(1)}, bf16[192,2304]{1,0:T(8,128)(2,1)}, u32[]{:S(2)}) copy-start(bf16[192,2304]{1,0:T(8,128)(2,1)} %copy-done.8) | copy-start | bytes 2654212
  1241.2 28.9 %copy-start.17 = (bf16[192,4608]{1,0:T(8,128)(2,1)S(1)}, bf16[192,4608]{1,0:T(8,128)(2,1)}, u32[]{:S(2)}) copy-start(bf16[192,4608]{1,0:T(8,128)(2,1)} %get-tuple-element.105) | copy-start | bytes 5308420
  1241.2 1453.5 %reduce-scatter.17.cloned.1.call-start = ((), (), s32[]{:S(2)}) async-start(), calls=%async_computation.24 | async-start | bytes 135364608 | tf_op jit(solution)/shard_map/reduce_scatter | solution.py:229
  1242.3 27.8 %copy-start.18 = (bf16[192,4608]{1,0:T(8,128)(2,1)S(1)}, bf16[192,4608]{1,0:T(8,128)(2,1)}, u32[]{:S(2)}) copy-start(bf16[192,4608]{1,0:T(8,128)(2,1)} %get-tuple-element.106) | copy-start | bytes 5308420
  1388.3 1.0 copy-start.28
  1388.3 2.4 copy-start.38
  1388.3 2.4 copy-start.39
  1388.3 2.4 copy-start.40
  1388.3 45.4 %copy-start.4 = (f32[96,2304]{1,0:T(8,128)S(1)}, f32[96,2304]{1,0:T(8,128)}, u32[]{:S(2)}) copy-start(f32[96,2304]{1,0:T(8,128)} %copy-done.3) | copy-start | bytes 2654212
  (4 other events, 3.8 us)
Sparse Core Ops, SparseCore 0:
  10.3 45.2 all-gather.16
  57.8 41.0 all-gather.14
  101.3 51.8 all-gather.18
  155.3 51.6 all-gather.20
  212.4 26.8 reduce-scatter.8
  240.7 110.0 all-gather.22
  352.4 109.9 all-gather.24
  464.0 109.9 all-gather.26
  586.8 28.2 reduce-scatter.10
  620.9 109.9 all-gather.28
  732.6 109.9 all-gather.30
  844.0 109.9 all-gather.32
  967.3 28.2 reduce-scatter.12
  997.8 53.1 all-gather.34
  1053.1 51.6 all-gather.36
  1106.9 40.8 all-gather.38
  1150.0 41.0 all-gather.40
  1194.7 17.3 reduce-scatter.14
  1241.3 271.5 reduce-scatter.18
  1517.0 1177.6 reduce-scatter.16
where the time goes:
time: 2720 us; the launch traced here: 2710 us
  waiting for transfers between devices  2170 us (80%)
  matrix products  189 us (7%)
  blocking collectives  151 us (6%)
  other arithmetic  127 us (5%)
  local copies, waits for them, and re-layouts  54.3 us (2%)
    reduce_scatter x1, waiting for transfers between devices, shards(): lax.psum_scatter(jnp.concatenate([contract_first(left_rows, gate_up_grad)...  1180 us
    all_gather x1, waiting for transfers between devices, shards(): lax.all_gather(up_weight, 'fsdp', axis=0, tiled=True)  100 us
    all_gather x1, waiting for transfers between devices, shards(): lax.all_gather(held_back[5], 'fsdp', axis=0, tiled=True)  98.8 us
    all_gather x1, waiting for transfers between devices, shards(): lax.all_gather(held_back[4], 'fsdp', axis=0, tiled=True)  97.4 us
    all_gather x1, waiting for transfers between devices, shards(): lax.all_gather(down_weight, 'fsdp', axis=0, tiled=True)  96.9 us
    all_gather x1, waiting for transfers between devices, shards(): lax.all_gather(held_back[6], 'fsdp', axis=0, tiled=True)  95.9 us
    all_gather x1, waiting for transfers between devices, shards(): lax.all_gather(gate_weight, 'fsdp', axis=0, tiled=True)  95.7 us
    concatenate x1, other arithmetic, shards(): jnp.concatenate([contract_first(left_rows, gate_up_grad), contract_first(...  85.6 us
  transfers between devices with their start and end apart: 20, of which 18 were waited for; matrix products, arithmetic and copies ran while one was open for 12% of the time, Pallas kernels for 0%

commit v1 on v0

--- a/solution.py
+++ b/solution.py
@@ -8,6 +8,22 @@
 EPSILON = 1e-06
 SOFTCAP = 50.0
 NEGATIVE = -1e30
+
+
+def gather_around(x, axis, dim):
+    ways, here, step = (lax.axis_size(axis), lax.axis_index(axis), x.shape[dim])
+    shape = [n * ways if d == dim else n for d, n in enumerate(x.shape)]
+    full = lax.dynamic_update_slice_in_dim(jnp.zeros(shape, x.dtype), x, here * step, axis=dim)
+    going_up = going_down = x
+    for far in range(1, ways // 2 + 1):
+        going_up = lax.ppermute(going_up, axis, [(d, (d + 1) % ways) for d in range(ways)])
+        full = lax.dynamic_update_slice_in_dim(full, going_up, (here - far) % ways * step, axis=dim)
+        if 2 * far < ways:
+            going_down = lax.ppermute(going_down, axis, [(d, (d - 1) % ways) for d in range(ways)])
+            full = lax.dynamic_update_slice_in_dim(
+                full, going_down, (here + far) % ways * step, axis=dim
+            )
+    return full
 
 
 def contract_last(left_rows, right_rows):
@@ -127,7 +143,7 @@
         lax.all_gather(attention_post_gain, "fsdp", axis=0, tiled=True),
     )
     gate_full, up_full, down_full, gain_three, gain_four = (
-        lax.all_gather(gate_weight, "fsdp", axis=0, tiled=True),
+        gather_around(gate_weight, "fsdp", 0),
         lax.all_gather(up_weight, "fsdp", axis=0, tiled=True),
         lax.all_gather(down_weight, "fsdp", axis=0, tiled=True),
         lax.all_gather(feedforward_norm_gain, "fsdp", axis=0, tiled=True),

time: 2720 us -> 2810 us (1.033)
  starting transfers between devices: 0.99 us -> 281 us
  waiting for transfers between devices: 2170 us -> 1950 us
  local copies, waits for them, and re-layouts: 54.3 us -> 89.2 us
    ppermute x0 -> x15, starting transfers between devices: none -> 280 us  [the longest x8 275 us: gather_around(): lax.ppermute(going_up, axis, [(d, (d + 1) % ways) for d in range(ways)])]
    all_gather x1, waiting for transfers between devices: 100 us -> 0.01 us  [shards(): lax.all_gather(up_weight, 'fsdp', axis=0, tiled=True)]
    all_gather x1, waiting for transfers between devices: 96.9 us -> 0.01 us  [shards(): lax.all_gather(down_weight, 'fsdp', axis=0, tiled=True)]
    all_gather x1 -> x0, waiting for transfers between devices: 95.7 us -> none  [shards(): lax.all_gather(gate_weight, 'fsdp', axis=0, tiled=True)]
    ppermute x0 -> x15, waiting for transfers between devices: none -> 82.3 us  [the longest x8 82.3 us: gather_around(): lax.ppermute(going_up, axis, [(d, (d + 1) % ways) for d in range(ways)])]
    unnamed x21 -> x20, waiting for transfers between devices: 84.9 us -> 84.1 us
  transfers between devices with their start and end apart: 20 -> 34, of which waited for: 18 -> 21; matrix products, arithmetic and copies ran while one was open for 12% -> 13% of each run, Pallas kernels for 0% -> 0%
where the time goes in v1:
time: 2810 us; the launch traced here: 2800 us
  waiting for transfers between devices  1950 us (69%)
  starting transfers between devices  281 us (10%)
  matrix products  190 us (7%)
  blocking collectives  148 us (5%)
  other arithmetic  127 us (5%)
  local copies, waits for them, and re-layouts  89.2 us (3%)
    reduce_scatter x1, waiting for transfers between devices, shards(): lax.psum_scatter(jnp.concatenate([contract_first(left_rows, gate_up_grad)...  1180 us
    ppermute x8, starting transfers between devices, gather_around(): lax.ppermute(going_up, axis, [(d, (d + 1) % ways) for d in range(ways)])  275 us
    all_gather x1, waiting for transfers between devices, shards(): lax.all_gather(held_back[5], 'fsdp', axis=0, tiled=True)  99 us
    all_gather x1, waiting for transfers between devices, shards(): lax.all_gather(held_back[4], 'fsdp', axis=0, tiled=True)  97.2 us
    all_gather x1, waiting for transfers between devices, shards(): lax.all_gather(held_back[6], 'fsdp', axis=0, tiled=True)  96.2 us
    concatenate x1, other arithmetic, shards(): jnp.concatenate([contract_first(left_rows, gate_up_grad), contract_first(...  85.8 us
    unnamed x20, waiting for transfers between devices  84.1 us
    ppermute x8, waiting for transfers between devices, gather_around(): lax.ppermute(going_up, axis, [(d, (d + 1) % ways) for d in range(ways)])  82.3 us
  transfers between devices with their start and end apart: 34, of which 21 were waited for; matrix products, arithmetic and copies ran while one was open for 13% of the time, Pallas kernels for 0%

profile of v1, /device:TPU:0, one launch (start us, length us, event | category | flops | bytes accessed | tf_op | source)
XLA Modules:
  0.0 2802.7 jit_solution(16302443292058600138)
XLA Ops:
  15.4 63.9 %all-reduce.5 = (bf16[2304]{0:T(1024)(128)(2,1)S(1)}, bf16[2304]{0:T(1024)(128)(2,1)S(1)}, bf16[2304]{0:T(1024)(128)(2,1)S(1)}, bf16[2304]{0:T(1024)(128)(2,1)S(1)}) all-reduce(bf16[2304]{0:T(1024)(128)(2,1)S(1)} %dynamic-update-slice, bf16[2304]{0:T(1024)(128)(2,1)S(1)} %dynamic-update-slice.1, ...), channel_id=1, replica_groups=mesh['fsdp'=16,'tp'=2] {'fsdp'}, use_global_device_ids=true, to_apply=%add | all-reduce | flops 9216 | bytes 36864
  83.3 9.0 all_gather.64
  93.0 2.3 fusion.107
  95.6 3.4 all-gather.14.cloned.1.call-done
  101.6 51.6 %all-gather.18.cloned.1.call-done = bf16[2304,1024]{1,0:T(8,128)(2,1)} async-done(((bf16[144,1024]{1,0:T(8,128)(2,1)}), bf16[2304,1024]{1,0:T(8,128)(2,1)}) %all-gather.18.cloned.1.call-update) | async-done | bytes 4718608 | tf_op jit(solution)/shard_map/all_gather | solution.py:138
  153.2 3.4 fusion.108
  159.3 47.7 %all-gather.20.cloned.1.call-done = bf16[2304,1024]{1,0:T(8,128)(2,1)} async-done(((bf16[144,1024]{1,0:T(8,128)(2,1)}), bf16[2304,1024]{1,0:T(8,128)(2,1)}) %all-gather.20.cloned.1.call-update) | async-done | bytes 4718608 | tf_op jit(solution)/shard_map/all_gather | solution.py:141
  207.0 5.2 fusion.109
  214.0 4.2 collective-permute-start.1
  218.1 15.6 collective-permute-done
  233.7 9.6 collective-permute-start.2
  244.4 12.3 collective-permute-done.2
  256.7 51.6 %collective-permute-start.4 = (bf16[144,4608]{1,0:T(8,128)(2,1)}, bf16[144,4608]{1,0:T(8,128)(2,1)}, u32[]{:S(2)}, u32[]{:S(2)}) collective-permute-start(bf16[144,4608]{1,0:T(8,128)(2,1)} %collective-permute-done.2), channel_id=1, source_target_pairs={{0,2},{2,4},{4,6},{6,8},{8,10},{10,12},{12,14},{14,16},{16,18},{18... | collective-permute-start | bytes 3981320 | tf_op jit(solution)/shard_map/ppermute | solution.py:19
  308.3 17.1 collective-permute-done.4
  325.5 42.7 %collective-permute-start.6 = (bf16[144,4608]{1,0:T(8,128)(2,1)}, bf16[144,4608]{1,0:T(8,128)(2,1)}, u32[]{:S(2)}, u32[]{:S(2)}) collective-permute-start(bf16[144,4608]{1,0:T(8,128)(2,1)} %collective-permute-done.4), channel_id=1, source_target_pairs={{0,2},{2,4},{4,6},{6,8},{8,10},{10,12},{12,14},{14,16},{16,18},{18... | collective-permute-start | bytes 3981320 | tf_op jit(solution)/shard_map/ppermute | solution.py:19
  368.2 7.3 broadcast_in_dim.44
  376.8 2.6 constant_dynamic-update-slice_fusion.13
  380.5 15.0 collective-permute-done.6
  395.5 39.8 %collective-permute-start.8 = (bf16[144,4608]{1,0:T(8,128)(2,1)}, bf16[144,4608]{1,0:T(8,128)(2,1)S(1)}, u32[]{:S(2)}, u32[]{:S(2)}) collective-permute-start(bf16[144,4608]{1,0:T(8,128)(2,1)} %collective-permute-done.6), channel_id=1, source_target_pairs={{0,2},{2,4},{4,6},{6,8},{8,10},{10,12},{12,14},{14,16},{16,18},{18... | collective-permute-start | bytes 3981320 | tf_op jit(solution)/shard_map/ppermute | solution.py:19
  435.3 2.5 constant_dynamic-update-slice_fusion.11
  437.8 2.5 constant_dynamic-update-slice_fusion.10
  440.3 2.4 constant_dynamic-update-slice_fusion.9
  442.7 45.6 %collective-permute-start.10 = (bf16[144,4608]{1,0:T(8,128)(2,1)S(1)}, bf16[144,4608]{1,0:T(8,128)(2,1)S(1)}, u32[]{:S(2)}, u32[]{:S(2)}) collective-permute-start(bf16[144,4608]{1,0:T(8,128)(2,1)S(1)} %collective-permute-done.8), channel_id=1, source_target_pairs={{0,2},{2,4},{4,6},{6,8},{8,10},{10,12},{12,14},{14,16},{16,18},{18... | collective-permute-start | bytes 3981320 | tf_op jit(solution)/shard_map/ppermute | solution.py:19
  488.3 2.5 constant_dynamic-update-slice_fusion.8
  490.8 2.6 constant_dynamic-update-slice_fusion.7
  494.5 10.1 collective-permute-done.10
  504.6 43.5 %collective-permute-start.12 = (bf16[144,4608]{1,0:T(8,128)(2,1)S(1)}, bf16[144,4608]{1,0:T(8,128)(2,1)S(1)}, u32[]{:S(2)}, u32[]{:S(2)}) collective-permute-start(bf16[144,4608]{1,0:T(8,128)(2,1)S(1)} %collective-permute-done.10), channel_id=1, source_target_pairs={{0,2},{2,4},{4,6},{6,8},{8,10},{10,12},{12,14},{14,16},{16,18},{18... | collective-permute-start | bytes 3981320 | tf_op jit(solution)/shard_map/ppermute | solution.py:19
  551.8 42.3 %collective-permute-start.14 = (bf16[144,4608]{1,0:T(8,128)(2,1)S(1)}, bf16[144,4608]{1,0:T(8,128)(2,1)S(1)}, u32[]{:S(2)}, u32[]{:S(2)}) collective-permute-start(bf16[144,4608]{1,0:T(8,128)(2,1)S(1)} %collective-permute-done.12), channel_id=1, source_target_pairs={{0,2},{2,4},{4,6},{6,8},{8,10},{10,12},{12,14},{14,16},{16,18},{18... | collective-permute-start | bytes 3981320 | tf_op jit(solution)/shard_map/ppermute | solution.py:19
  597.5 12.0 collective-permute-done.14
  613.7 9.0 all_gather.71
  622.7 11.9 fusion.110
  634.6 14.7 multiply_convert_fusion.1
  649.3 12.6 fusion.111
  662.1 48.0 %reduce-scatter.11.cloned.1.call-done = f32[96,2304]{1,0:T(8,128)} async-done(((f32[192,2304]{1,0:T(8,128)}), f32[96,2304]{1,0:T(8,128)}) %reduce-scatter.11.cloned.1.call-update) | async-done | bytes 884752 | tf_op jit(solution)/shard_map/reduce_scatter | solution.py:203
  717.1 12.6 all_gather.75
  729.7 96.2 %all-gather.26.cloned.1.call-done = bf16[2304,4608]{1,0:T(8,128)(2,1)} async-done(((bf16[144,4608]{1,0:T(8,128)(2,1)}), bf16[2304,4608]{1,0:T(8,128)(2,1)}) %all-gather.26.cloned.1.call-update) | async-done | bytes 21233680 | tf_op jit(solution)/shard_map/all_gather | solution.py:232
  825.9 14.2 multiply_convert_fusion
  840.1 97.2 %all-gather.28.cloned.1.call-done = bf16[2304,4608]{1,0:T(8,128)(2,1)} async-done(((bf16[144,4608]{1,0:T(8,128)(2,1)}), bf16[2304,4608]{1,0:T(8,128)(2,1)}) %all-gather.28.cloned.1.call-update) | async-done | bytes 21233680 | tf_op jit(solution)/shard_map/all_gather | solution.py:230
  937.3 12.6 fusion.112
  950.0 99.0 %all-gather.30.cloned.1.call-done = bf16[2304,4608]{1,0:T(8,128)(2,1)} async-done(((bf16[144,4608]{1,0:T(8,128)(2,1)}), bf16[2304,4608]{1,0:T(8,128)(2,1)}) %all-gather.30.cloned.1.call-update) | async-done | bytes 21233680 | tf_op jit(solution)/shard_map/all_gather | solution.py:231
  1049.0 13.1 convolution_add_fusion.2
  1064.6 25.9 reduce-scatter.13.cloned.1.call-done
  1095.7 12.7 all_gather.79
  1108.4 37.6 %all-gather.32.cloned.1.call-done = bf16[2304,1024]{1,0:T(8,128)(2,1)} async-done(((bf16[144,1024]{1,0:T(8,128)(2,1)}), bf16[2304,1024]{1,0:T(8,128)(2,1)}) %all-gather.32.cloned.1.call-update) | async-done | bytes 4718608 | tf_op jit(solution)/shard_map/all_gather | solution.py:229
  1146.0 4.2 convolution_convert_fusion
  1156.9 3.1 fusion.39
  1162.0 37.8 %all-gather.34.cloned.1.call-done = bf16[2304,1024]{1,0:T(8,128)(2,1)} async-done(((bf16[144,1024]{1,0:T(8,128)(2,1)}), bf16[2304,1024]{1,0:T(8,128)(2,1)}) %all-gather.34.cloned.1.call-update) | async-done | bytes 4718608 | tf_op jit(solution)/shard_map/all_gather | solution.py:226
  1199.8 5.3 fusion.113
  1205.1 37.8 %all-gather.36.cloned.1.call-done = bf16[2304,512]{1,0:T(8,128)(2,1)} async-done(((bf16[144,512]{1,0:T(8,128)(2,1)}), bf16[2304,512]{1,0:T(8,128)(2,1)}) %all-gather.36.cloned.1.call-update) | async-done | bytes 2359312 | tf_op jit(solution)/shard_map/all_gather | solution.py:227
  1242.9 3.2 convolution_add_fusion.1
  1246.1 5.0 fusion.114
  1251.1 8.0 fusion.44
  1259.2 26.9 all-gather.38.cloned.1.call-done
  1286.1 3.5 fusion.1
  1289.6 18.9 pad_maximum_fusion.1
  1308.5 27.7 copy.111
  1337.4 27.8 fusion.115
  1365.2 32.5 %fusion.9 = f32[2304,9216]{1,0:T(8,128)} fusion(bf16[192,2304]{1,0:T(8,128)(2,1)S(1)} %copy-done.10, bf16[192,4608]{1,0:T(8,128)(2,1)S(1)} %copy-done.18, bf16[192,4608]{1,0:T(8,128)(2,1)S(1)} %copy-done.19), kind=kOutput, calls=%fused_computation.16 | convolution fusion | flops 8160804864 | bytes 89358336 | tf_op jit(solution)/shard_map/dot_general | solution.py:36
  1397.7 85.8 %pad_maximum_fusion = f32[2304,13824]{1,0:T(8,128)} fusion(f32[2304,4608]{1,0:T(8,128)} %fusion.115, f32[2304,9216]{1,0:T(8,128)} %fusion.9), kind=kLoop, calls=%fused_computation.1 | loop fusion | flops 31850496 | bytes 254803968 | tf_op jit(solution)/shard_map/concatenate | solution.py:246
  1486.1 40.5 %all-reduce.4 = (f32[2304]{0:T(1024)S(1)}, f32[2304]{0:T(1024)S(1)}, f32[2304]{0:T(1024)S(1)}, f32[2304]{0:T(1024)S(1)}) all-reduce(f32[2304]{0:T(1024)S(1)} %get-tuple-element.87, f32[2304]{0:T(1024)S(1)} %copy-done.44, f32[2304]{0:T(1024)S(1)} %copy-done.43, f32[2304]{0:T(1024)S(1)} %copy-done.42), channel_id=1, replica_groups=mesh['fsdp'=16,'tp'=2] {'fsdp','tp'}, use_global_device_ids=true, to_apply=%region_19.20 | all-reduce | flops 9216 | bytes 73728 | tf_op jit(solution)/shard_map/psum | solution.py:336
  1531.3 76.7 %reduce-scatter.19.cloned.1.call-done = f32[144,3072]{1,0:T(8,128)} async-done(((f32[2304,3072]{1,0:T(8,128)}), f32[144,3072]{1,0:T(8,128)}) %reduce-scatter.19.cloned.1.call-update) | async-done | bytes 1769488
  1609.9 2.4 fusion.103
  1612.3 1176.6 %reduce-scatter.17.cloned.1.call-done = f32[144,13824]{1,0:T(8,128)} async-done(((f32[2304,13824]{1,0:T(8,128)}), f32[144,13824]{1,0:T(8,128)}) %reduce-scatter.17.cloned.1.call-update) | async-done | bytes 7962640 | tf_op jit(solution)/shard_map/reduce_scatter | solution.py:245
  2788.9 6.8 fusion.102
  (248 shorter events, 68.6 us)
Async XLA Ops:
  7.2 85.1 %copy-start.51 = (s32[1,9]{1,0:T(1,128)S(1)}, s32[1,9]{1,0:T(1,128)}, u32[]{:S(2)}) copy-start(s32[1,9]{1,0:T(1,128)} %param.15) | copy-start | bytes 112
  7.2 85.8 %all-gather.16.cloned.1.call-start = ((), (), s32[]{:S(2)}) async-start(), calls=%async_computation.7 | async-start | bytes 2506752 | tf_op jit(solution)/shard_map/all_gather | solution.py:139
  7.9 91.1 %all-gather.14.cloned.1.call-start = ((), (), s32[]{:S(2)}) async-start(), calls=%async_computation.6 | async-start | bytes 2506752 | tf_op jit(solution)/shard_map/all_gather | solution.py:140
  8.7 144.5 %all-gather.18.cloned.1.call-start = ((), (), s32[]{:S(2)}) async-start(), calls=%async_computation.8 | async-start | bytes 5013504 | tf_op jit(solution)/shard_map/all_gather | solution.py:138
  9.4 197.6 %all-gather.20.cloned.1.call-start = ((), (), s32[]{:S(2)}) async-start(), calls=%async_computation.9 | async-start | bytes 5013504 | tf_op jit(solution)/shard_map/all_gather | solution.py:141
  10.0 600.7 %reduce-scatter.9.cloned.1.call-start = ((), (), s32[]{:S(2)}) async-start(), calls=%async_computation.10 | async-start | bytes 2654208 | tf_op jit(solution)/shard_map/reduce_scatter | solution.py:191
  79.2 13.7 copy-start.31
  82.1 13.4 copy-start.45
  92.5 65.4 %copy-start.33 = (pred[192,192]{0,1:T(8,128)(4,1)}, pred[192,192]{0,1:T(8,128)(4,1)S(1)}, u32[]{:S(2)}) copy-start(pred[192,192]{0,1:T(8,128)(4,1)S(1)} %fusion.77) | copy-start | bytes 110596
  92.9 64.0 %copy-start.11 = (f32[192,128]{1,0:T(8,128)}, f32[192,128]{1,0:T(8,128)S(1)}, u32[]{:S(2)}) copy-start(f32[192,128]{1,0:T(8,128)S(1)} %get-tuple-element.125) | copy-start | bytes 294916
  92.9 64.0 %copy-start.13 = (f32[192,128]{1,0:T(8,128)}, f32[192,128]{1,0:T(8,128)S(1)}, u32[]{:S(2)}) copy-start(f32[192,128]{1,0:T(8,128)S(1)} %get-tuple-element.126) | copy-start | bytes 294916
  101.3 56.6 %copy-start.29 = (bf16[192,2,256]{2,1,0:T(2,128)(2,1)}, bf16[192,2,256]{2,1,0:T(2,128)(2,1)S(1)}, u32[]{:S(2)}) copy-start(bf16[192,2,256]{2,1,0:T(2,128)(2,1)S(1)} %reshape.267) | copy-start | bytes 589828
  101.6 55.7 %copy-start.39 = (bf16[192,2,128]{2,0,1:T(8,128)(2,1)}, bf16[192,2,128]{2,0,1:T(8,128)(2,1)S(1)}, u32[]{:S(2)}) copy-start(bf16[192,2,128]{2,0,1:T(8,128)(2,1)S(1)} %get-tuple-element.121) | copy-start | bytes 294916
  101.6 55.7 %copy-start.41 = (bf16[192,2,128]{2,0,1:T(8,128)(2,1)}, bf16[192,2,128]{2,0,1:T(8,128)(2,1)S(1)}, u32[]{:S(2)}) copy-start(bf16[192,2,128]{2,0,1:T(8,128)(2,1)S(1)} %get-tuple-element.122) | copy-start | bytes 294916
  157.9 54.3 %copy-start.49 = (f32[2,2,192]{2,1,0:T(2,128)}, f32[2,2,192]{2,1,0:T(2,128)S(1)}, u32[]{:S(2)}) copy-start(f32[2,2,192]{2,1,0:T(2,128)S(1)} %log_add_fusion) | copy-start | bytes 9220
  159.2 47.8 %copy-start.20 = (bf16[192,1024]{1,0:T(8,128)(2,1)}, bf16[192,1024]{1,0:T(8,128)(2,1)S(1)}, u32[]{:S(2)}) copy-start(bf16[192,1024]{1,0:T(8,128)(2,1)S(1)} %convert_element_type.109) | copy-start | bytes 1179652
  212.3 422.3 %all-gather.22.cloned.1.call-start = ((), (), s32[]{:S(2)}) async-start(), calls=%async_computation.11 | async-start | bytes 22560768 | tf_op jit(solution)/shard_map/all_gather | solution.py:147
  212.8 436.5 %all-gather.24.cloned.1.call-start = ((), (), s32[]{:S(2)}) async-start(), calls=%async_computation.12 | async-start | bytes 22560768 | tf_op jit(solution)/shard_map/all_gather | solution.py:148
  213.6 496.4 %reduce-scatter.11.cloned.1.call-start = ((), (), s32[]{:S(2)}) async-start(), calls=%async_computation.13 | async-start | bytes 2654208 | tf_op jit(solution)/shard_map/reduce_scatter | solution.py:203
  213.7 20.1 collective-permute-start
  214.0 29.4 %collective-permute-start.1 = (bf16[144,4608]{1,0:T(8,128)(2,1)S(1)}, bf16[144,4608]{1,0:T(8,128)(2,1)S(1)}, u32[]{:S(2)}, u32[]{:S(2)}) collective-permute-start(bf16[144,4608]{1,0:T(8,128)(2,1)S(1)} %copy-done.5), channel_id=1, source_target_pairs={{0,30},{2,0},{4,2},{6,4},{8,6},{10,8},{12,10},{14,12},{16,14},{18,... | collective-permute-start | bytes 3981320 | tf_op jit(solution)/shard_map/ppermute | solution.py:22
  233.7 74.6 %copy-start.26 = (bf16[144,4608]{1,0:T(8,128)(2,1)}, bf16[144,4608]{1,0:T(8,128)(2,1)S(1)}, u32[]{:S(2)}) copy-start(bf16[144,4608]{1,0:T(8,128)(2,1)S(1)} %collective-permute-done) | copy-start | bytes 3981316
  233.7 23.0 collective-permute-start.2
  244.4 63.9 %collective-permute-start.3 = (bf16[144,4608]{1,0:T(8,128)(2,1)S(1)}, bf16[144,4608]{1,0:T(8,128)(2,1)}, u32[]{:S(2)}, u32[]{:S(2)}) collective-permute-start(bf16[144,4608]{1,0:T(8,128)(2,1)S(1)} %collective-permute-done.1), channel_id=1, source_target_pairs={{0,30},{2,0},{4,2},{6,4},{8,6},{10,8},{12,10},{14,12},{16,14},{18,... | collective-permute-start | bytes 3981320 | tf_op jit(solution)/shard_map/ppermute | solution.py:22
  256.7 68.8 %collective-permute-start.4 = (bf16[144,4608]{1,0:T(8,128)(2,1)}, bf16[144,4608]{1,0:T(8,128)(2,1)}, u32[]{:S(2)}, u32[]{:S(2)}) collective-permute-start(bf16[144,4608]{1,0:T(8,128)(2,1)} %collective-permute-done.2), channel_id=1, source_target_pairs={{0,2},{2,4},{4,6},{6,8},{8,10},{10,12},{12,14},{14,16},{16,18},{18... | collective-permute-start | bytes 3981320 | tf_op jit(solution)/shard_map/ppermute | solution.py:19
  308.3 71.0 %collective-permute-start.5 = (bf16[144,4608]{1,0:T(8,128)(2,1)}, bf16[144,4608]{1,0:T(8,128)(2,1)}, u32[]{:S(2)}, u32[]{:S(2)}) collective-permute-start(bf16[144,4608]{1,0:T(8,128)(2,1)} %collective-permute-done.3), channel_id=1, source_target_pairs={{0,30},{2,0},{4,2},{6,4},{8,6},{10,8},{12,10},{14,12},{16,14},{18,... | collective-permute-start | bytes 3981320 | tf_op jit(solution)/shard_map/ppermute | solution.py:22
  325.5 70.1 %collective-permute-start.6 = (bf16[144,4608]{1,0:T(8,128)(2,1)}, bf16[144,4608]{1,0:T(8,128)(2,1)}, u32[]{:S(2)}, u32[]{:S(2)}) collective-permute-start(bf16[144,4608]{1,0:T(8,128)(2,1)} %collective-permute-done.4), channel_id=1, source_target_pairs={{0,2},{2,4},{4,6},{6,8},{8,10},{10,12},{12,14},{14,16},{16,18},{18... | collective-permute-start | bytes 3981320 | tf_op jit(solution)/shard_map/ppermute | solution.py:19
  376.7 236.9 %copy-start.37 = (f32[2304]{0:T(1024)}, f32[2304]{0:T(1024)S(1)}, u32[]{:S(2)}) copy-start(f32[2304]{0:T(1024)S(1)} %convert_element_type.111) | copy-start | bytes 27652
  379.4 60.9 %collective-permute-start.7 = (bf16[144,4608]{1,0:T(8,128)(2,1)}, bf16[144,4608]{1,0:T(8,128)(2,1)S(1)}, u32[]{:S(2)}, u32[]{:S(2)}) collective-permute-start(bf16[144,4608]{1,0:T(8,128)(2,1)} %collective-permute-done.5), channel_id=1, source_target_pairs={{0,30},{2,0},{4,2},{6,4},{8,6},{10,8},{12,10},{14,12},{16,14},{18,... | collective-permute-start | bytes 3981320 | tf_op jit(solution)/shard_map/ppermute | solution.py:22
  395.5 47.2 %collective-permute-start.8 = (bf16[144,4608]{1,0:T(8,128)(2,1)}, bf16[144,4608]{1,0:T(8,128)(2,1)S(1)}, u32[]{:S(2)}, u32[]{:S(2)}) collective-permute-start(bf16[144,4608]{1,0:T(8,128)(2,1)} %collective-permute-done.6), channel_id=1, source_target_pairs={{0,2},{2,4},{4,6},{6,8},{8,10},{10,12},{12,14},{14,16},{16,18},{18... | collective-permute-start | bytes 3981320 | tf_op jit(solution)/shard_map/ppermute | solution.py:19
  440.2 53.1 %collective-permute-start.9 = (bf16[144,4608]{1,0:T(8,128)(2,1)S(1)}, bf16[144,4608]{1,0:T(8,128)(2,1)S(1)}, u32[]{:S(2)}, u32[]{:S(2)}) collective-permute-start(bf16[144,4608]{1,0:T(8,128)(2,1)S(1)} %collective-permute-done.7), channel_id=1, source_target_pairs={{0,30},{2,0},{4,2},{6,4},{8,6},{10,8},{12,10},{14,12},{16,14},{18,... | collective-permute-start | bytes 3981320 | tf_op jit(solution)/shard_map/ppermute | solution.py:22
  442.7 61.9 %collective-permute-start.10 = (bf16[144,4608]{1,0:T(8,128)(2,1)S(1)}, bf16[144,4608]{1,0:T(8,128)(2,1)S(1)}, u32[]{:S(2)}, u32[]{:S(2)}) collective-permute-start(bf16[144,4608]{1,0:T(8,128)(2,1)S(1)} %collective-permute-done.8), channel_id=1, source_target_pairs={{0,2},{2,4},{4,6},{6,8},{8,10},{10,12},{12,14},{14,16},{16,18},{18... | collective-permute-start | bytes 3981320 | tf_op jit(solution)/shard_map/ppermute | solution.py:19
  493.3 57.2 %collective-permute-start.11 = (bf16[144,4608]{1,0:T(8,128)(2,1)S(1)}, bf16[144,4608]{1,0:T(8,128)(2,1)S(1)}, u32[]{:S(2)}, u32[]{:S(2)}) collective-permute-start(bf16[144,4608]{1,0:T(8,128)(2,1)S(1)} %collective-permute-done.9), channel_id=1, source_target_pairs={{0,30},{2,0},{4,2},{6,4},{8,6},{10,8},{12,10},{14,12},{16,14},{18,... | collective-permute-start | bytes 3981320 | tf_op jit(solution)/shard_map/ppermute | solution.py:22
  504.6 47.2 %collective-permute-start.12 = (bf16[144,4608]{1,0:T(8,128)(2,1)S(1)}, bf16[144,4608]{1,0:T(8,128)(2,1)S(1)}, u32[]{:S(2)}, u32[]{:S(2)}) collective-permute-start(bf16[144,4608]{1,0:T(8,128)(2,1)S(1)} %collective-permute-done.10), channel_id=1, source_target_pairs={{0,2},{2,4},{4,6},{6,8},{8,10},{10,12},{12,14},{14,16},{16,18},{18... | collective-permute-start | bytes 3981320 | tf_op jit(solution)/shard_map/ppermute | solution.py:19
  550.5 45.8 %collective-permute-start.13 = (bf16[144,4608]{1,0:T(8,128)(2,1)S(1)}, bf16[144,4608]{1,0:T(8,128)(2,1)S(1)}, u32[]{:S(2)}, u32[]{:S(2)}) collective-permute-start(bf16[144,4608]{1,0:T(8,128)(2,1)S(1)} %collective-permute-done.11), channel_id=1, source_target_pairs={{0,30},{2,0},{4,2},{6,4},{8,6},{10,8},{12,10},{14,12},{16,14},{18,... | collective-permute-start | bytes 3981320 | tf_op jit(solution)/shard_map/ppermute | solution.py:22
  551.8 57.7 %collective-permute-start.14 = (bf16[144,4608]{1,0:T(8,128)(2,1)S(1)}, bf16[144,4608]{1,0:T(8,128)(2,1)S(1)}, u32[]{:S(2)}, u32[]{:S(2)}) collective-permute-start(bf16[144,4608]{1,0:T(8,128)(2,1)S(1)} %collective-permute-done.12), channel_id=1, source_target_pairs={{0,2},{2,4},{4,6},{6,8},{8,10},{10,12},{12,14},{14,16},{16,18},{18... | collective-permute-start | bytes 3981320 | tf_op jit(solution)/shard_map/ppermute | solution.py:19
  596.4 15.7 copy-start.1
  622.7 11.9 copy-start.9
  649.3 62.1 %copy-start.8 = (bf16[96,2304]{1,0:T(8,128)(2,1)S(1)}, bf16[96,2304]{1,0:T(8,128)(2,1)}, u32[]{:S(2)}) copy-start(bf16[96,2304]{1,0:T(8,128)(2,1)} %param.27) | copy-start | bytes 1327108
  662.0 163.9 %all-gather.26.cloned.1.call-start = ((), (), s32[]{:S(2)}) async-start(), calls=%async_computation.14 | async-start | bytes 22560768 | tf_op jit(solution)/shard_map/all_gather | solution.py:232
  715.7 221.6 %all-gather.28.cloned.1.call-start = ((), (), s32[]{:S(2)}) async-start(), calls=%async_computation.15 | async-start | bytes 22560768 | tf_op jit(solution)/shard_map/all_gather | solution.py:230
  716.3 332.7 %all-gather.30.cloned.1.call-start = ((), (), s32[]{:S(2)}) async-start(), calls=%async_computation.16 | async-start | bytes 22560768 | tf_op jit(solution)/shard_map/all_gather | solution.py:231
  717.0 373.5 %reduce-scatter.13.cloned.1.call-start = ((), (), s32[]{:S(2)}) async-start(), calls=%async_computation.17 | async-start | bytes 2654208 | tf_op jit(solution)/shard_map/reduce_scatter | solution.py:255
  729.7 110.4 %copy-start.6 = (bf16[192,2304]{1,0:T(8,128)(2,1)}, bf16[192,2304]{1,0:T(8,128)(2,1)S(1)}, u32[]{:S(2)}) copy-start(bf16[192,2304]{1,0:T(8,128)(2,1)S(1)} %all_gather.75) | copy-start | bytes 2654212
  1049.0 41.6 %copy-start.38 = (f32[2304]{0:T(1024)S(1)}, f32[2304]{0:T(1024)}, u32[]{:S(2)}) copy-start(f32[2304]{0:T(1024)} %copy-done.37) | copy-start | bytes 27652
  1062.1 30.5 %copy-start = (f32[96,2304]{1,0:T(8,128)S(1)}, f32[96,2304]{1,0:T(8,128)}, u32[]{:S(2)}) copy-start(f32[96,2304]{1,0:T(8,128)} %reduce-scatter.9.cloned.1.call-done) | copy-start | bytes 2654212
  1062.1 30.5 %copy-start.48 = (f32[96]{0:T(128)S(1)}, f32[96]{0:T(128)}, u32[]{:S(2)}) copy-start(f32[96]{0:T(128)} %copy-done.47) | copy-start | bytes 1156
  1062.1 83.9 %all-gather.32.cloned.1.call-start = ((), (), s32[]{:S(2)}) async-start(), calls=%async_computation.18 | async-start | bytes 5013504 | tf_op jit(solution)/shard_map/all_gather | solution.py:229
  1062.9 137.0 %all-gather.34.cloned.1.call-start = ((), (), s32[]{:S(2)}) async-start(), calls=%async_computation.19 | async-start | bytes 5013504 | tf_op jit(solution)/shard_map/all_gather | solution.py:226
  1063.4 179.4 %all-gather.36.cloned.1.call-start = ((), (), s32[]{:S(2)}) async-start(), calls=%async_computation.20 | async-start | bytes 2506752 | tf_op jit(solution)/shard_map/all_gather | solution.py:227
  1064.0 222.0 %all-gather.38.cloned.1.call-start = ((), (), s32[]{:S(2)}) async-start(), calls=%async_computation.21 | async-start | bytes 2506752 | tf_op jit(solution)/shard_map/all_gather | solution.py:228
  1064.6 419.1 %reduce-scatter.15.cloned.1.call-start = ((), (), s32[]{:S(2)}) async-start(), calls=%async_computation.22 | async-start | bytes 1327104 | tf_op jit(solution)/shard_map/reduce_scatter | solution.py:326
  1108.4 43.1 %copy-start.28 = (f32[2,192,192,2]{2,1,3,0:T(8,128)S(1)}, f32[2,192,192,2]{2,1,3,0:T(8,128)}, u32[]{:S(2)}) copy-start(f32[2,192,192,2]{2,1,3,0:T(8,128)} %copy-done.27) | copy-start | bytes 1769476
  1108.4 43.1 %copy-start.34 = (pred[192,192]{0,1:T(8,128)(4,1)S(1)}, pred[192,192]{0,1:T(8,128)(4,1)}, u32[]{:S(2)}) copy-start(pred[192,192]{0,1:T(8,128)(4,1)} %copy-done.33) | copy-start | bytes 110596
  1108.4 43.1 %copy-start.50 = (f32[2,2,192]{2,1,0:T(2,128)S(1)}, f32[2,2,192]{2,1,0:T(2,128)}, u32[]{:S(2)}) copy-start(f32[2,2,192]{2,1,0:T(2,128)} %copy-done.49) | copy-start | bytes 9220
  1108.4 44.2 %copy-start.30 = (bf16[192,2,256]{2,1,0:T(2,128)(2,1)S(1)}, bf16[192,2,256]{2,1,0:T(2,128)(2,1)}, u32[]{:S(2)}) copy-start(bf16[192,2,256]{2,1,0:T(2,128)(2,1)} %copy-done.29) | copy-start | bytes 589828
  1162.0 43.1 %copy-start.22 = (bf16[24,8,4,256]{3,1,2,0:T(8,128)(2,1)}, bf16[24,8,4,256]{3,1,2,0:T(8,128)(2,1)S(1)}, u32[]{:S(2)}) copy-start(bf16[24,8,4,256]{3,1,2,0:T(8,128)(2,1)S(1)} %copy.123) | copy-start | bytes 1179652
  1251.1 34.9 %copy-start.16 = (bf16[2,24,8,256]{3,2,0,1:T(8,128)(2,1)S(1)}, bf16[2,24,8,256]{3,2,0,1:T(8,128)(2,1)}, u32[]{:S(2)}) copy-start(bf16[2,24,8,256]{3,2,0,1:T(8,128)(2,1)} %copy.122) | copy-start | bytes 589828
  1289.6 318.4 %reduce-scatter.19.cloned.1.call-start = ((), (), s32[]{:S(2)}) async-start(), calls=%async_computation.24 | async-start | bytes 30081024
  1336.3 28.9 %copy-start.10 = (bf16[192,2304]{1,0:T(8,128)(2,1)S(1)}, bf16[192,2304]{1,0:T(8,128)(2,1)}, u32[]{:S(2)}) copy-start(bf16[192,2304]{1,0:T(8,128)(2,1)} %copy-done.9) | copy-start | bytes 2654212
  1336.3 28.9 %copy-start.18 = (bf16[192,4608]{1,0:T(8,128)(2,1)S(1)}, bf16[192,4608]{1,0:T(8,128)(2,1)}, u32[]{:S(2)}) copy-start(bf16[192,4608]{1,0:T(8,128)(2,1)} %get-tuple-element.105) | copy-start | bytes 5308420
  1336.3 1452.6 %reduce-scatter.17.cloned.1.call-start = ((), (), s32[]{:S(2)}) async-start(), calls=%async_computation.23 | async-start | bytes 135364608 | tf_op jit(solution)/shard_map/reduce_scatter | solution.py:245
  1337.4 27.8 copy-start.19
  1483.6 45.5 %copy-start.4 = (f32[96,2304]{1,0:T(8,128)S(1)}, f32[96,2304]{1,0:T(8,128)}, u32[]{:S(2)}) copy-start(f32[96,2304]{1,0:T(8,128)} %copy-done.3) | copy-start | bytes 2654212
  (22 other events, 54.6 us)
Sparse Core Ops, SparseCore 0:
  10.3 45.2 all-gather.15
  57.8 41.0 all-gather.13
  101.3 51.8 all-gather.17
  155.3 51.6 all-gather.19
  212.4 26.8 reduce-scatter.8
  240.7 208.0 all-gather.21
  450.4 184.2 all-gather.23
  662.1 47.8 reduce-scatter.10
  715.8 110.0 all-gather.25
  827.3 109.9 all-gather.27
  938.9 109.9 all-gather.29
  1062.2 28.2 reduce-scatter.12
  1092.8 53.1 all-gather.31
  1148.1 51.6 all-gather.33
  1202.0 40.8 all-gather.35
  1245.0 41.0 all-gather.37
  1289.7 17.3 reduce-scatter.14
  1336.4 271.5 reduce-scatter.18
  1612.3 1176.6 reduce-scatter.16
